TPU v7x, 32 devices: a whole 2x2x4 slice. The times are simulated.
32 devices in a mesh: groups: 2 (over y), ctx: 4 (over z), role: 2 (over x), seq: 2 (over core).
Axes of the slice: x: 2, y: 2, z: 4, core: 2. Of those that a mesh axis runs over, the one named last changes fastest.
Arguments:
- queries: bfloat16 [32, 128, 576], P(('groups', 'role', 'seq'), 'ctx'), parts along dimension 0, may hold values from -24 to 24
- cache: bfloat16 [16, 4096, 576], P(('groups', 'role', 'seq'), 'ctx'), parts along dimension 0, may hold values from -4 to 4
- lengths: int32 [16], P(('groups', 'role', 'seq')), parts along dimension 0, may hold values from 4 to 4096, as said below
- positions: int32 [32], P(('groups', 'role', 'seq')), parts along dimension 0, may hold values from 0 to 4098, as said below
- value_up_weight: bfloat16 [128, 512, 128], P('ctx', ('role', 'seq')), may hold values from -0.25 to 0.25
- out_proj: bfloat16 [16384, 7168], P('ctx', ('role', 'seq')), may hold values from -0.046875 to 0.046875
- residual: bfloat16 [32, 7168], P('groups', ('role', 'seq')), parts along dimension 0, may hold values from -4 to 4
- norm_gain: float32 [7168], P(('role', 'seq')), may hold values from 0.5 to 1.5
- gate_weight: bfloat16 [7168, 9216], P(('role', 'seq'), 'ctx'), may hold values from -0.0625 to 0.0625
- up_weight: bfloat16 [7168, 9216], P(('role', 'seq'), 'ctx'), may hold values from -0.0625 to 0.0625
- down_weight: bfloat16 [9216, 7168], P('ctx', ('role', 'seq')), may hold values from -0.0625 to 0.0625
Outputs:
- layer_out: bfloat16 [32, 7168], P(('groups', 'ctx'), ('role', 'seq')), parts along dimension 0
There are 2 independent parts, one for each index of `groups`. A program takes and returns all parts, laid end to end along the dimension named above; an argument that names none is the same for every part. Nothing has to cross between parts.
Inputs may be any that keep to these rules, and one draw needn't show every extreme that they name: `lengths`: every sequence has at least 4 cached positions, and in every draw some sequence has all 4096. positions[r] lies between lengths[r // 2] - 4 and lengths[r // 2] + 2.
All inputs are finite; a program needn't handle non-finite values.
Results may differ from a plain program's by a relative error of at most 0.013.
Values may be sent and summed in bfloat16 or wider, within the bound.
A program may use at most 128 MiB of HBM per device.

v0:
```python
import jax
import jax.numpy as jnp
from jax import lax
from jax.sharding import PartitionSpec as P

D = 7168
HEADS = 128
LATENT = 512
ROPE = 64
VDIM = 128
MTP = 2
softmax_scale = 0.07216878364870323
epsilon = 1e-06


def settle_heads(pieces):
    maxima, totals, partial_value = pieces
    highest = jnp.max(maxima, axis=0)
    factor = jnp.exp(maxima - highest[None])
    denom = jnp.sum(factor * totals, axis=0)
    numer = jnp.sum(factor[..., None] * partial_value, axis=0)
    return (numer / denom[..., None]).astype(jnp.bfloat16)


def per_device(
    queries,
    cache,
    lengths,
    positions,
    value_up_weight,
    out_proj,
    residual,
    norm_gain,
    gate_weight,
    up_weight,
    down_weight,
):
    all_heads = lax.all_gather(queries, "ctx", axis=1, tiled=True)
    heads_here = queries.shape[1]
    width = LATENT + ROPE
    context_local = cache.shape[1]
    seq_here = cache.shape[0]
    offset = lax.axis_index("ctx") * context_local
    places = offset + jnp.arange(context_local, dtype=jnp.int32)
    maxima_list = []
    totals_list = []
    partial_list = []
    for number in range(seq_here):
        rows_pair = all_heads[MTP * number : MTP * (number + 1)].reshape(MTP * HEADS, width)
        keys_here = cache[number]
        limits = jnp.repeat(positions[MTP * number : MTP * (number + 1)], HEADS)
        length = lengths[number]

        def compute_block(rows_pair=rows_pair, keys_here=keys_here, limits=limits, length=length):
            scores = (
                jnp.dot(rows_pair, keys_here.T, preferred_element_type=jnp.float32) * softmax_scale
            )
            live = (places[None, :] < length) & (places[None, :] <= limits[:, None])
            block_max = jnp.max(jnp.where(live, scores, jnp.float32(-1e30)), axis=-1)
            probs = jnp.exp(
                jnp.where(live, scores - block_max[:, None], jnp.float32(-1e30))
            ).astype(jnp.bfloat16)
            block_weight_sum = jnp.sum(probs.astype(jnp.float32), axis=-1)
            block_out = jnp.dot(probs, keys_here[:, :LATENT], preferred_element_type=jnp.float32)
            return (block_max, block_weight_sum, block_out)

        block_max, block_weight_sum, block_out = compute_block()
        maxima_list.append(block_max.reshape(MTP, HEADS))
        totals_list.append(block_weight_sum.reshape(MTP, HEADS))
        partial_list.append(block_out.reshape(MTP, HEADS, LATENT))
    maxima = jnp.concatenate(maxima_list, axis=0)
    totals = jnp.concatenate(totals_list, axis=0)
    partial_value = jnp.concatenate(partial_list, axis=0)
    attended_values = settle_heads(
        (
            lax.all_to_all(maxima[None], "ctx", split_axis=2, concat_axis=0, tiled=True),
            lax.all_to_all(totals[None], "ctx", split_axis=2, concat_axis=0, tiled=True),
            lax.all_to_all(partial_value[None], "ctx", split_axis=2, concat_axis=0, tiled=True),
        )
    )
    mixed = jnp.einsum(
        "nut,utc->nuc",
        attended_values,
        lax.all_gather(value_up_weight, ("role", "seq"), axis=1, tiled=True),
        preferred_element_type=jnp.float32,
    )
    value_vectors = mixed.astype(jnp.bfloat16).reshape(attended_values.shape[0], heads_here * VDIM)
    per_head_terms = jnp.dot(
        lax.all_gather(value_vectors, ("role", "seq"), axis=0, tiled=True),
        out_proj,
        preferred_element_type=jnp.float32,
    )
    attn_out = lax.psum(per_head_terms, "ctx")
    resid = residual.astype(jnp.float32) + attn_out
    sumsq = lax.psum(jnp.sum(resid * resid, axis=1), ("role", "seq"))
    normed = (resid * lax.rsqrt(sumsq / D + epsilon)[:, None] * norm_gain[None, :]).astype(
        jnp.bfloat16
    )
    gate_term = jnp.dot(normed, gate_weight, preferred_element_type=jnp.float32)
    up_term = jnp.dot(normed, up_weight, preferred_element_type=jnp.float32)
    gate, up = lax.psum((gate_term, up_term), ("role", "seq"))
    hidden = (jax.nn.silu(gate) * up).astype(jnp.bfloat16)
    rows_here = resid.shape[0] // lax.axis_size("ctx")
    ffn_rows = lax.psum_scatter(
        jnp.dot(hidden, down_weight, preferred_element_type=jnp.float32),
        "ctx",
        scatter_dimension=0,
        tiled=True,
    )
    base_rows = lax.dynamic_slice_in_dim(resid, lax.axis_index("ctx") * rows_here, rows_here, 0)
    return (base_rows + ffn_rows).astype(jnp.bfloat16)


def solution(mesh):
    placed = (
        P(("groups", "role", "seq"), "ctx", None),
        P(("groups", "role", "seq"), "ctx", None),
        P(("groups", "role", "seq")),
        P(("groups", "role", "seq")),
        P("ctx", ("role", "seq"), None),
        P("ctx", ("role", "seq")),
        P("groups", ("role", "seq")),
        P(("role", "seq")),
        P(("role", "seq"), "ctx"),
        P(("role", "seq"), "ctx"),
        P("ctx", ("role", "seq")),
    )
    return jax.shard_map(
        per_device,
        mesh=mesh,
        in_specs=placed,
        out_specs=P(("groups", "ctx"), ("role", "seq")),
        check_vma=False,
    )
```

profile of v0, /device:TPU:0, one launch (start us, length us, event | category | flops | bytes accessed | tf_op | source)
XLA Modules:
  0.0 227.1 jit_solution(11326140525146923370)
XLA Ops:
  6.5 0.0 all-gather.3.cloned.1.call-start
  6.5 0.7 all-gather.3.cloned.1.call-update
  7.3 1.3 fusion.19
  8.6 1.3 fusion.12
  9.9 19.9 %all_gather.9 = bf16[4,128,576]{2,1,0:T(8,128)(2,1)S(1)} all-gather(bf16[4,32,576]{2,1,0:T(8,128)(2,1)} %param.11), channel_id=1, replica_groups=mesh['groups'=2,'ctx'=4,'role'=2,'seq'=2] {'ctx'}, dimensions={1}, use_global_device_ids=true | all-gather | bytes 737280 | tf_op jit(solution)/shard_map/all_gather | solution.py:38
  29.8 0.8 fusion.20
  30.6 0.1 broadcast_bitcast_fusion
  30.7 0.1 fusion.18
  30.7 1.8 convolution_multiply_fusion
  32.6 0.0 copy-done
  32.6 0.9 select_reduce_fusion.1
  33.5 0.9 convert_reduce_fusion.1
  34.4 0.1 copy.23
  34.5 0.6 broadcast.49
  35.1 0.8 reduce.1
  35.9 0.7 reshape.68
  36.6 3.8 %all-to-all-start.2 = ((f32[4,1,128]{2,1,0:T(1,128)}), f32[4,1,128]{2,1,0:T(1,128)S(1)}, u32[]{:S(2)}, u32[]{:S(2)}) async-start(f32[4,1,128]{2,1,0:T(1,128)} %reshape.68), calls=%async_computation.2 | async-start | bytes 4096 | tf_op jit(solution)/shard_map/all_to_all | solution.py:77
  40.4 0.2 slice_bitcast_fusion.1
  40.6 0.5 fusion.3
  41.1 0.5 fusion.1
  41.6 0.1 copy.18
  41.7 0.8 reduce.3
  42.5 0.7 reshape.66
  43.2 0.4 copy.20
  43.6 0.4 copy.21
  44.0 1.9 all-to-all-done.2
  45.9 3.2 %all-to-all-start = ((f32[4,1,128]{2,1,0:T(1,128)}), f32[4,1,128]{2,1,0:T(1,128)S(1)}, u32[]{:S(2)}, u32[]{:S(2)}) async-start(f32[4,1,128]{2,1,0:T(1,128)} %reshape.66), calls=%async_computation | async-start | bytes 4096 | tf_op jit(solution)/shard_map/all_to_all | solution.py:76
  49.1 1.4 maximum_bitcast_fusion
  50.6 4.1 %all-to-all-done = f32[4,1,128]{2,1,0:T(1,128)S(1)} async-done(((f32[4,1,128]{2,1,0:T(1,128)}), f32[4,1,128]{2,1,0:T(1,128)S(1)}, u32[]{:S(2)}, u32[]{:S(2)}) %all-to-all-start) | async-done | bytes 2080 | tf_op jit(solution)/shard_map/all_to_all | solution.py:76
  54.7 3.5 %all-to-all-start.1 = ((f32[1,4,128,512]{3,1,0,2:T(4,128)}), f32[1,4,128,512]{3,1,0,2:T(4,128)S(1)}, u32[]{:S(2)}, u32[]{:S(2)}) async-start(f32[1,4,128,512]{3,1,0,2:T(4,128)} %maximum_bitcast_fusion), calls=%async_computation.1 | async-start | bytes 2097152 | tf_op jit(solution)/shard_map/all_to_all | solution.py:78
  58.2 0.0 all-reduce.6.cloned.1.call-start
  58.3 0.7 reduce.2
  58.9 0.1 reshape.69
  59.1 0.1 copy.24
  59.2 0.7 reduce.4
  59.8 0.1 reshape.67
  60.0 0.1 copy.19
  60.1 18.8 %all-to-all-done.1 = f32[1,4,128,512]{3,1,0,2:T(4,128)S(1)} async-done(((f32[1,4,128,512]{3,1,0,2:T(4,128)}), f32[1,4,128,512]{3,1,0,2:T(4,128)S(1)}, u32[]{:S(2)}, u32[]{:S(2)}) %all-to-all-start.1) | async-done | bytes 1048608 | tf_op jit(solution)/shard_map/all_to_all | solution.py:78
  78.9 0.3 fusion.5
  79.3 0.1 divide_convert_fusion
  79.4 0.0 all-gather.3.cloned.1.call-done
  79.4 2.8 %fusion = bf16[1,4,4096]{2,1,0:T(4,128)(2,1)S(1)} fusion(bf16[32,512,128]{2,1,0:T(8,128)(2,1)} %all-gather.3.cloned.1.call-done, bf16[4,32,512]{2,1,0:T(8,128)(2,1)S(1)} %divide_convert_fusion), kind=kOutput, calls=%fused_computation.5 | convolution fusion | flops 16793600 | bytes 4358144 | tf_op jit(solution)/shard_map/nut,utc->nuc/dot_general | solution.py:81
  82.2 5.4 %all-gather = bf16[4,4,4096]{2,1,0:T(4,128)(2,1)S(1)} all-gather(bf16[1,4,4096]{2,1,0:T(4,128)(2,1)S(1)} %fusion), channel_id=1, replica_groups=mesh['groups'=2,'ctx'=4,'role'=2,'seq'=2] {'role','seq'}, dimensions={0}, use_global_device_ids=true | all-gather | bytes 163840 | tf_op jit(solution)/shard_map/all_gather | solution.py:89
  87.7 0.0 copy-start.2
  87.7 0.0 copy-start.1
  87.7 7.8 %fusion.21 = f32[16,1792]{1,0:T(8,128)} fusion(bf16[16,4096]{1,0:T(8,128)(2,1)S(1)} %reshape.63, bf16[4096,1792]{1,0:T(8,128)(2,1)} %param.16), kind=kOutput, calls=%fused_computation.50 | convolution fusion | flops 234881024 | bytes 14925824 | tf_op jit(solution)/shard_map/dot_general | solution.py:88
  95.5 0.0 all-reduce.6.cloned.1.call-update
  95.6 0.0 all-reduce.10.cloned.1.call-start
  95.6 33.5 %all-reduce.6.cloned.1.call-done = f32[16,1792]{1,0:T(8,128)} async-done(((f32[16,1792]{1,0:T(8,128)}), f32[16,1792]{1,0:T(8,128)}) %all-reduce.6.cloned.1.call-update) | async-done | bytes 114704 | tf_op jit(solution)/shard_map/psum | solution.py:93
  129.1 0.0 copy-done.2
  129.1 1.0 multiply_reduce_fusion
  130.1 5.7 %psum.29 = f32[16]{0:T(128)S(1)} all-reduce(f32[16]{0:T(128)S(1)} %get-tuple-element.9), channel_id=1, replica_groups=mesh['groups'=2,'ctx'=4,'role'=2,'seq'=2] {'role','seq'}, use_global_device_ids=true, to_apply=%region_9.10 | all-reduce | flops 16 | bytes 128 | tf_op jit(solution)/shard_map/psum | solution.py:95
  135.8 0.0 copy-done.1
  135.8 5.2 %fusion.16 = f32[16,2304]{1,0:T(8,128)} fusion(bf16[1792,2304]{1,0:T(8,128)(2,1)} %param.19, f32[16,1792]{1,0:T(8,128)S(1)} %get-tuple-element.10, f32[1792]{0:T(1024)S(1)} %copy-done.1, f32[16]{0:T(128)S(1)} %add_rsqrt_fusion), kind=kOutput, calls=%fused_computation.46 | convolution fusion | flops 132206592 | bytes 8526912 | tf_op jit(solution)/shard_map/dot_general | solution.py:99
  141.1 5.3 %fusion.15 = f32[16,2304]{1,0:T(8,128)} fusion(bf16[1792,2304]{1,0:T(8,128)(2,1)} %param.20, f32[16,1792]{1,0:T(8,128)S(1)} %get-tuple-element.10, f32[1792]{0:T(1024)S(1)} %copy-done.1, f32[16]{0:T(128)S(1)} %add_rsqrt_fusion), kind=kOutput, calls=%fused_computation.45 | convolution fusion | flops 132206592 | bytes 8526912 | tf_op jit(solution)/shard_map/dot_general | solution.py:100
  146.3 0.0 all-reduce.10.cloned.1.call-update
  146.3 0.0 all-reduce.8.cloned.1.call-start
  146.4 32.9 %all-reduce.10.cloned.1.call-done = (f32[16,2304]{1,0:T(8,128)}, f32[16,2304]{1,0:T(8,128)}) async-done(((f32[16,2304]{1,0:T(8,128)}, f32[16,2304]{1,0:T(8,128)}), (f32[16,2304]{1,0:T(8,128)}, f32[16,2304]{1,0:T(8,128)})) %all-reduce.10.cloned.1.call-update) | async-done | bytes 294928 | tf_op jit(solution)/shard_map/psum | solution.py:101
  179.2 5.4 %fusion.7 = f32[16,1792]{1,0:T(8,128)} fusion(bf16[2304,1792]{1,0:T(8,128)(2,1)} %param.21, f32[16,2304]{1,0:T(8,128)} %get-tuple-element.7, f32[16,2304]{1,0:T(8,128)} %get-tuple-element.8), kind=kOutput, calls=%fused_computation.27 | convolution fusion | flops 132341760 | bytes 8667136 | tf_op jit(solution)/shard_map/dot_general | solution.py:105
  184.6 0.0 all-reduce.8.cloned.1.call-update
  184.7 0.0 copy-done.3
  184.7 0.6 dynamic-slice
  185.9 33.3 %all-reduce.8.cloned.1.call-done = f32[16,1792]{1,0:T(8,128)} async-done(((f32[16,1792]{1,0:T(8,128)}), f32[16,1792]{1,0:T(8,128)}) %all-reduce.8.cloned.1.call-update) | async-done | bytes 114704
  219.2 1.4 fusion.9
  (9 shorter events, 0.1 us)
Async XLA Ops:
  6.5 26.1 %copy-start = (bf16[2,1024,576]{1,2,0:T(8,128)(2,1)S(1)}, bf16[2,1024,576]{1,2,0:T(8,128)(2,1)}, u32[]{:S(2)}) copy-start(bf16[2,1024,576]{1,2,0:T(8,128)(2,1)} %param.12) | copy-start | bytes 7077892
  6.5 72.8 %all-gather.3.cloned.1.call-start = ((), (), s32[]{:S(2)}) async-start(), calls=%async_computation.3 | async-start | bytes 5242880 | tf_op jit(solution)/shard_map/all_gather | solution.py:84
  36.6 9.3 %all-to-all-start.2 = ((f32[4,1,128]{2,1,0:T(1,128)}), f32[4,1,128]{2,1,0:T(1,128)S(1)}, u32[]{:S(2)}, u32[]{:S(2)}) async-start(f32[4,1,128]{2,1,0:T(1,128)} %reshape.68), calls=%async_computation.2 | async-start | bytes 4096 | tf_op jit(solution)/shard_map/all_to_all | solution.py:77
  45.9 8.8 %all-to-all-start = ((f32[4,1,128]{2,1,0:T(1,128)}), f32[4,1,128]{2,1,0:T(1,128)S(1)}, u32[]{:S(2)}, u32[]{:S(2)}) async-start(f32[4,1,128]{2,1,0:T(1,128)} %reshape.66), calls=%async_computation | async-start | bytes 4096 | tf_op jit(solution)/shard_map/all_to_all | solution.py:76
  54.7 24.2 %all-to-all-start.1 = ((f32[1,4,128,512]{3,1,0,2:T(4,128)}), f32[1,4,128,512]{3,1,0,2:T(4,128)S(1)}, u32[]{:S(2)}, u32[]{:S(2)}) async-start(f32[1,4,128,512]{3,1,0,2:T(4,128)} %maximum_bitcast_fusion), calls=%async_computation.1 | async-start | bytes 2097152 | tf_op jit(solution)/shard_map/all_to_all | solution.py:78
  58.2 70.9 %all-reduce.6.cloned.1.call-start = ((), (), s32[]{:S(2)}) async-start(), calls=%async_computation.4 | async-start | bytes 229376 | tf_op jit(solution)/shard_map/psum | solution.py:93
  87.7 41.4 %copy-start.2 = (bf16[16,1792]{1,0:T(8,128)(2,1)S(1)}, bf16[16,1792]{1,0:T(8,128)(2,1)}, u32[]{:S(2)}) copy-start(bf16[16,1792]{1,0:T(8,128)(2,1)} %param.17) | copy-start | bytes 172036
  87.7 48.1 %copy-start.1 = (f32[1792]{0:T(1024)S(1)}, f32[1792]{0:T(1024)}, u32[]{:S(2)}) copy-start(f32[1792]{0:T(1024)} %param.18) | copy-start | bytes 21508
  95.6 83.7 %all-reduce.10.cloned.1.call-start = ((), (), s32[]{:S(2)}) async-start(), calls=%async_computation.6 | async-start | bytes 589824 | tf_op jit(solution)/shard_map/psum | solution.py:101
  146.3 72.8 %all-reduce.8.cloned.1.call-start = ((), (), s32[]{:S(2)}) async-start(), calls=%async_computation.5 | async-start | bytes 229376
  179.2 5.4 %copy-start.3 = (u32[32]{0:T(128)S(1)}, u32[32]{0:T(128)}, u32[]{:S(2)}) copy-start(u32[32]{0:T(128)} %constant.35) | copy-start | bytes 388
Sparse Core Ops, SparseCore 0:
  8.9 37.1 all-gather.2
  95.7 33.3 all-reduce.5
  146.4 32.7 all-reduce.9
  184.8 34.3 all-reduce.7
where the time goes:
time: 228 us; the launch traced here: 227 us
  waiting for transfers between devices  125 us (55%)
  blocking collectives  31 us (14%)
  matrix products  30.3 us (13%)
  between operations  14 us (6%)
  starting transfers between devices  10.7 us (5%)
  other arithmetic  9.47 us (4%)
  local copies, waits for them, and re-layouts  6.56 us (3%)
    unnamed x5, waiting for transfers between devices  34 us
    psum x1, waiting for transfers between devices, per_device(): attn_out = lax.psum(per_head_terms, 'ctx')  33.5 us
    psum x1, waiting for transfers between devices, per_device(): gate, up = lax.psum((gate_term, up_term), ('role', 'seq'))  32.9 us
    all_gather x1, blocking collectives, per_device(): all_heads = lax.all_gather(queries, 'ctx', axis=1, tiled=True)  19.9 us
    all_to_all x1, waiting for transfers between devices, per_device(): lax.all_to_all(partial_value[None], 'ctx', split_axis=2, concat_axis=0, t...  18.8 us
    dot_general x1, matrix products, per_device(): jnp.dot(lax.all_gather(value_vectors, ('role', 'seq'), axis=0, tiled=True...  7.84 us
    psum x1, blocking collectives, per_device(): sumsq = lax.psum(jnp.sum(resid * resid, axis=1), ('role', 'seq'))  5.66 us
    all_gather x1, blocking collectives, per_device(): lax.all_gather(value_vectors, ('role', 'seq'), axis=0, tiled=True)  5.41 us
  transfers between devices with their start and end apart: 7, of which 6 were waited for; matrix products, arithmetic and copies ran while one was open for 8% of the time, Pallas kernels for 0%

commit v1 on v0

--- a/solution.py
+++ b/solution.py
@@ -98,7 +98,7 @@
     )
     gate_term = jnp.dot(normed, gate_weight, preferred_element_type=jnp.float32)
     up_term = jnp.dot(normed, up_weight, preferred_element_type=jnp.float32)
-    gate, up = lax.psum((gate_term, up_term), ("role", "seq"))
+    gate, up = lax.psum(lax.psum((gate_term, up_term), "seq"), axis_name="role")
     hidden = (jax.nn.silu(gate) * up).astype(jnp.bfloat16)
     rows_here = resid.shape[0] // lax.axis_size("ctx")
     ffn_rows = lax.psum_scatter(

time: 228 us -> 241 us (1.057)
  waiting for transfers between devices: 125 us -> 138 us
    psum x1 -> x2, waiting for transfers between devices: 32.9 us -> 45.8 us  [per_device(): gate, up = lax.psum(lax.psum((gate_term, up_term), 'seq'), axis_name='role')]
    unnamed x5 -> x6, waiting for transfers between devices: 34 us -> 34 us
  transfers between devices with their start and end apart: 7 -> 8, of which waited for: 6 -> 7; matrix products, arithmetic and copies ran while one was open for 8% -> 7% of each run, Pallas kernels for 0% -> 0%
where the time goes in v1:
time: 241 us; the launch traced here: 240 us
  waiting for transfers between devices  138 us (57%)
  blocking collectives  31 us (13%)
  matrix products  30.2 us (13%)
  between operations  14 us (6%)
  starting transfers between devices  10.7 us (4%)
  other arithmetic  9.47 us (4%)
  local copies, waits for them, and re-layouts  6.56 us (3%)
    psum x2, waiting for transfers between devices, per_device(): gate, up = lax.psum(lax.psum((gate_term, up_term), 'seq'), axis_name='role')  45.8 us
    unnamed x6, waiting for transfers between devices  34 us
    psum x1, waiting for transfers between devices, per_device(): attn_out = lax.psum(per_head_terms, 'ctx')  33.5 us
    all_gather x1, blocking collectives, per_device(): all_heads = lax.all_gather(queries, 'ctx', axis=1, tiled=True)  19.9 us
    all_to_all x1, waiting for transfers between devices, per_device(): lax.all_to_all(partial_value[None], 'ctx', split_axis=2, concat_axis=0, t...  18.8 us
    dot_general x1, matrix products, per_device(): jnp.dot(lax.all_gather(value_vectors, ('role', 'seq'), axis=0, tiled=True...  7.84 us
    psum x1, blocking collectives, per_device(): sumsq = lax.psum(jnp.sum(resid * resid, axis=1), ('role', 'seq'))  5.66 us
    all_gather x1, blocking collectives, per_device(): lax.all_gather(value_vectors, ('role', 'seq'), axis=0, tiled=True)  5.41 us
  transfers between devices with their start and end apart: 8, of which 7 were waited for; matrix products, arithmetic and copies ran while one was open for 7% of the time, Pallas kernels for 0%

profile of v1, /device:TPU:0, one launch (start us, length us, event | category | flops | bytes accessed | tf_op | source)
XLA Modules:
  0.0 240.1 jit_solution(9200819351560369629)
XLA Ops:
  6.5 0.0 all-gather.3.cloned.1.call-start
  6.5 0.7 all-gather.3.cloned.1.call-update
  7.3 1.3 fusion.19
  8.6 1.3 fusion.12
  9.9 19.9 %all_gather.9 = bf16[4,128,576]{2,1,0:T(8,128)(2,1)S(1)} all-gather(bf16[4,32,576]{2,1,0:T(8,128)(2,1)} %param.11), channel_id=1, replica_groups=mesh['groups'=2,'ctx'=4,'role'=2,'seq'=2] {'ctx'}, dimensions={1}, use_global_device_ids=true | all-gather | bytes 737280 | tf_op jit(solution)/shard_map/all_gather | solution.py:38
  29.8 0.8 fusion.20
  30.6 0.1 broadcast_bitcast_fusion
  30.7 0.1 fusion.18
  30.7 1.8 convolution_multiply_fusion
  32.6 0.9 select_reduce_fusion.1
  33.5 0.9 convert_reduce_fusion.1
  34.4 0.1 copy.23
  34.5 0.6 broadcast.49
  35.1 0.8 reduce.1
  35.9 0.7 reshape.68
  36.6 3.8 %all-to-all-start.2 = ((f32[4,1,128]{2,1,0:T(1,128)}), f32[4,1,128]{2,1,0:T(1,128)S(1)}, u32[]{:S(2)}, u32[]{:S(2)}) async-start(f32[4,1,128]{2,1,0:T(1,128)} %reshape.68), calls=%async_computation.2 | async-start | bytes 4096 | tf_op jit(solution)/shard_map/all_to_all | solution.py:77
  40.4 0.2 slice_bitcast_fusion.1
  40.6 0.5 fusion.3
  41.1 0.5 fusion.1
  41.6 0.1 copy.18
  41.7 0.8 reduce.3
  42.5 0.7 reshape.66
  43.2 0.4 copy.20
  43.6 0.4 copy.21
  44.0 1.9 all-to-all-done.2
  45.9 3.2 %all-to-all-start = ((f32[4,1,128]{2,1,0:T(1,128)}), f32[4,1,128]{2,1,0:T(1,128)S(1)}, u32[]{:S(2)}, u32[]{:S(2)}) async-start(f32[4,1,128]{2,1,0:T(1,128)} %reshape.66), calls=%async_computation | async-start | bytes 4096 | tf_op jit(solution)/shard_map/all_to_all | solution.py:76
  49.1 1.4 maximum_bitcast_fusion
  50.6 4.1 %all-to-all-done = f32[4,1,128]{2,1,0:T(1,128)S(1)} async-done(((f32[4,1,128]{2,1,0:T(1,128)}), f32[4,1,128]{2,1,0:T(1,128)S(1)}, u32[]{:S(2)}, u32[]{:S(2)}) %all-to-all-start) | async-done | bytes 2080 | tf_op jit(solution)/shard_map/all_to_all | solution.py:76
  54.7 3.5 %all-to-all-start.1 = ((f32[1,4,128,512]{3,1,0,2:T(4,128)}), f32[1,4,128,512]{3,1,0,2:T(4,128)S(1)}, u32[]{:S(2)}, u32[]{:S(2)}) async-start(f32[1,4,128,512]{3,1,0,2:T(4,128)} %maximum_bitcast_fusion), calls=%async_computation.1 | async-start | bytes 2097152 | tf_op jit(solution)/shard_map/all_to_all | solution.py:78
  58.2 0.0 all-reduce.8.cloned.1.call-start
  58.3 0.7 reduce.2
  58.9 0.1 reshape.69
  59.1 0.1 copy.24
  59.2 0.7 reduce.4
  59.8 0.1 reshape.67
  60.0 0.1 copy.19
  60.1 18.8 %all-to-all-done.1 = f32[1,4,128,512]{3,1,0,2:T(4,128)S(1)} async-done(((f32[1,4,128,512]{3,1,0,2:T(4,128)}), f32[1,4,128,512]{3,1,0,2:T(4,128)S(1)}, u32[]{:S(2)}, u32[]{:S(2)}) %all-to-all-start.1) | async-done | bytes 1048608 | tf_op jit(solution)/shard_map/all_to_all | solution.py:78
  78.9 0.3 fusion.5
  79.3 0.1 divide_convert_fusion
  79.4 0.0 all-gather.3.cloned.1.call-done
  79.4 2.8 %fusion = bf16[1,4,4096]{2,1,0:T(4,128)(2,1)S(1)} fusion(bf16[32,512,128]{2,1,0:T(8,128)(2,1)} %all-gather.3.cloned.1.call-done, bf16[4,32,512]{2,1,0:T(8,128)(2,1)S(1)} %divide_convert_fusion), kind=kOutput, calls=%fused_computation.5 | convolution fusion | flops 16793600 | bytes 4358144 | tf_op jit(solution)/shard_map/nut,utc->nuc/dot_general | solution.py:81
  82.2 5.4 %all-gather = bf16[4,4,4096]{2,1,0:T(4,128)(2,1)S(1)} all-gather(bf16[1,4,4096]{2,1,0:T(4,128)(2,1)S(1)} %fusion), channel_id=1, replica_groups=mesh['groups'=2,'ctx'=4,'role'=2,'seq'=2] {'role','seq'}, dimensions={0}, use_global_device_ids=true | all-gather | bytes 163840 | tf_op jit(solution)/shard_map/all_gather | solution.py:89
  87.7 0.0 copy-start.2
  87.7 0.0 copy-start.1
  87.7 7.8 %fusion.21 = f32[16,1792]{1,0:T(8,128)} fusion(bf16[16,4096]{1,0:T(8,128)(2,1)S(1)} %reshape.63, bf16[4096,1792]{1,0:T(8,128)(2,1)} %param.16), kind=kOutput, calls=%fused_computation.50 | convolution fusion | flops 234881024 | bytes 14925824 | tf_op jit(solution)/shard_map/dot_general | solution.py:88
  95.5 0.0 all-reduce.8.cloned.1.call-update
  95.6 0.0 all-reduce.12.cloned.1.call-start
  95.6 33.5 %all-reduce.8.cloned.1.call-done = f32[16,1792]{1,0:T(8,128)} async-done(((f32[16,1792]{1,0:T(8,128)}), f32[16,1792]{1,0:T(8,128)}) %all-reduce.8.cloned.1.call-update) | async-done | bytes 114704 | tf_op jit(solution)/shard_map/psum | solution.py:93
  129.1 1.0 multiply_reduce_fusion
  130.1 5.7 %psum.43 = f32[16]{0:T(128)S(1)} all-reduce(f32[16]{0:T(128)S(1)} %get-tuple-element.11), channel_id=1, replica_groups=mesh['groups'=2,'ctx'=4,'role'=2,'seq'=2] {'role','seq'}, use_global_device_ids=true, to_apply=%region_9.10 | all-reduce | flops 16 | bytes 128 | tf_op jit(solution)/shard_map/psum | solution.py:95
  135.8 0.0 copy-done.1
  135.8 5.2 %fusion.16 = f32[16,2304]{1,0:T(8,128)} fusion(bf16[1792,2304]{1,0:T(8,128)(2,1)} %param.19, f32[16,1792]{1,0:T(8,128)S(1)} %get-tuple-element.12, f32[1792]{0:T(1024)S(1)} %copy-done.1, f32[16]{0:T(128)S(1)} %add_rsqrt_fusion), kind=kOutput, calls=%fused_computation.46 | convolution fusion | flops 132206592 | bytes 8526912 | tf_op jit(solution)/shard_map/dot_general | solution.py:99
  141.1 5.3 %fusion.15 = f32[16,2304]{1,0:T(8,128)} fusion(bf16[1792,2304]{1,0:T(8,128)(2,1)} %param.20, f32[16,1792]{1,0:T(8,128)S(1)} %get-tuple-element.12, f32[1792]{0:T(1024)S(1)} %copy-done.1, f32[16]{0:T(128)S(1)} %add_rsqrt_fusion), kind=kOutput, calls=%fused_computation.45 | convolution fusion | flops 132206592 | bytes 8526912 | tf_op jit(solution)/shard_map/dot_general | solution.py:100
  146.3 0.0 all-reduce.12.cloned.1.call-update
  146.3 0.0 all-reduce.14.cloned.1.call-start
  146.4 18.7 %all-reduce.12.cloned.1.call-done = (f32[16,2304]{1,0:T(8,128)}, f32[16,2304]{1,0:T(8,128)}) async-done(((f32[16,2304]{1,0:T(8,128)}, f32[16,2304]{1,0:T(8,128)}), (f32[16,2304]{1,0:T(8,128)}, f32[16,2304]{1,0:T(8,128)})) %all-reduce.12.cloned.1.call-update) | async-done | bytes 294928 | tf_op jit(solution)/shard_map/psum | solution.py:101
  165.1 0.0 all-reduce.14.cloned.1.call-update
  165.1 0.0 all-reduce.10.cloned.1.call-start
  165.2 27.1 %all-reduce.14.cloned.1.call-done = (f32[16,2304]{1,0:T(8,128)}, f32[16,2304]{1,0:T(8,128)}) async-done(((f32[16,2304]{1,0:T(8,128)}, f32[16,2304]{1,0:T(8,128)}), (f32[16,2304]{1,0:T(8,128)}, f32[16,2304]{1,0:T(8,128)})) %all-reduce.14.cloned.1.call-update) | async-done | bytes 294928 | tf_op jit(solution)/shard_map/psum | solution.py:101
  192.3 5.4 %fusion.7 = f32[16,1792]{1,0:T(8,128)} fusion(bf16[2304,1792]{1,0:T(8,128)(2,1)} %param.21, f32[16,2304]{1,0:T(8,128)} %get-tuple-element.9, f32[16,2304]{1,0:T(8,128)} %get-tuple-element.10), kind=kOutput, calls=%fused_computation.27 | convolution fusion | flops 132341760 | bytes 8667136 | tf_op jit(solution)/shard_map/dot_general | solution.py:105
  197.7 0.0 all-reduce.10.cloned.1.call-update
  197.7 0.6 dynamic-slice
  198.9 33.2 %all-reduce.10.cloned.1.call-done = f32[16,1792]{1,0:T(8,128)} async-done(((f32[16,1792]{1,0:T(8,128)}), f32[16,1792]{1,0:T(8,128)}) %all-reduce.10.cloned.1.call-update) | async-done | bytes 114704
  232.2 1.4 fusion.9
  (12 shorter events, 0.1 us)
Async XLA Ops:
  6.5 26.1 %copy-start = (bf16[2,1024,576]{1,2,0:T(8,128)(2,1)S(1)}, bf16[2,1024,576]{1,2,0:T(8,128)(2,1)}, u32[]{:S(2)}) copy-start(bf16[2,1024,576]{1,2,0:T(8,128)(2,1)} %param.12) | copy-start | bytes 7077892
  6.5 72.8 %all-gather.3.cloned.1.call-start = ((), (), s32[]{:S(2)}) async-start(), calls=%async_computation.3 | async-start | bytes 5242880 | tf_op jit(solution)/shard_map/all_gather | solution.py:84
  36.6 9.3 %all-to-all-start.2 = ((f32[4,1,128]{2,1,0:T(1,128)}), f32[4,1,128]{2,1,0:T(1,128)S(1)}, u32[]{:S(2)}, u32[]{:S(2)}) async-start(f32[4,1,128]{2,1,0:T(1,128)} %reshape.68), calls=%async_computation.2 | async-start | bytes 4096 | tf_op jit(solution)/shard_map/all_to_all | solution.py:77
  45.9 8.8 %all-to-all-start = ((f32[4,1,128]{2,1,0:T(1,128)}), f32[4,1,128]{2,1,0:T(1,128)S(1)}, u32[]{:S(2)}, u32[]{:S(2)}) async-start(f32[4,1,128]{2,1,0:T(1,128)} %reshape.66), calls=%async_computation | async-start | bytes 4096 | tf_op jit(solution)/shard_map/all_to_all | solution.py:76
  54.7 24.2 %all-to-all-start.1 = ((f32[1,4,128,512]{3,1,0,2:T(4,128)}), f32[1,4,128,512]{3,1,0,2:T(4,128)S(1)}, u32[]{:S(2)}, u32[]{:S(2)}) async-start(f32[1,4,128,512]{3,1,0,2:T(4,128)} %maximum_bitcast_fusion), calls=%async_computation.1 | async-start | bytes 2097152 | tf_op jit(solution)/shard_map/all_to_all | solution.py:78
  58.2 70.9 %all-reduce.8.cloned.1.call-start = ((), (), s32[]{:S(2)}) async-start(), calls=%async_computation.4 | async-start | bytes 229376 | tf_op jit(solution)/shard_map/psum | solution.py:93
  87.7 41.4 %copy-start.2 = (bf16[16,1792]{1,0:T(8,128)(2,1)S(1)}, bf16[16,1792]{1,0:T(8,128)(2,1)}, u32[]{:S(2)}) copy-start(bf16[16,1792]{1,0:T(8,128)(2,1)} %param.17) | copy-start | bytes 172036
  87.7 48.1 %copy-start.1 = (f32[1792]{0:T(1024)S(1)}, f32[1792]{0:T(1024)}, u32[]{:S(2)}) copy-start(f32[1792]{0:T(1024)} %param.18) | copy-start | bytes 21508
  95.6 69.5 %all-reduce.12.cloned.1.call-start = ((), (), s32[]{:S(2)}) async-start(), calls=%async_computation.6 | async-start | bytes 589824 | tf_op jit(solution)/shard_map/psum | solution.py:101
  146.3 46.0 %all-reduce.14.cloned.1.call-start = ((), (), s32[]{:S(2)}) async-start(), calls=%async_computation.7 | async-start | bytes 589824 | tf_op jit(solution)/shard_map/psum | solution.py:101
  165.1 67.1 %all-reduce.10.cloned.1.call-start = ((), (), s32[]{:S(2)}) async-start(), calls=%async_computation.5 | async-start | bytes 229376
  192.3 5.4 %copy-start.3 = (u32[32]{0:T(128)S(1)}, u32[32]{0:T(128)}, u32[]{:S(2)}) copy-start(u32[32]{0:T(128)} %constant.35) | copy-start | bytes 388
Sparse Core Ops, SparseCore 0:
  8.9 37.1 all-gather.2
  95.7 33.3 all-reduce.7
  146.4 18.5 all-reduce.11
  167.3 24.9 all-reduce.13
  197.8 34.3 all-reduce.9
